TPU v7x, 16 devices: a 4x2x1 block of a 4x4x8 slice. The times are simulated.
16 devices in a mesh: dp: 2 (over y, z), tp: 8 (over x, core).
Axes of the slice: x: 4, y: 2, z: 1, core: 2. Of those that a mesh axis runs over, the one named last changes fastest.
The devices are a block of a 4x4x8 slice.
Arguments:
- x: bfloat16 [4096, 5120], P('dp'), parts along dimension 0
- w_gate: bfloat16 [5120, 16384], P(None, 'tp')
- w_up: bfloat16 [5120, 16384], P(None, 'tp')
- w_down: bfloat16 [16384, 5120], P('tp')
Outputs:
- output: bfloat16 [4096, 5120], P('dp'), parts along dimension 0
There are 2 independent parts. A program takes and returns all parts, laid end to end along the dimension named above; an argument that names none is the same for every part.
All inputs are finite; a program needn't handle non-finite values.
Results may differ from a plain program's by a relative error of at most 0.016.
Values are sent between devices in bfloat16 or wider.
A program may use at most 768 MiB of HBM per device.

v0:
```python
import jax
import jax.numpy as jnp
from jax import lax
from jax.sharding import PartitionSpec as P


def solution(mesh):
    def step(x, w_gate, w_up, w_down):
        gate = jnp.dot(x, w_gate, preferred_element_type=jnp.float32)
        up = jnp.dot(x, w_up, preferred_element_type=jnp.float32)
        hidden = (jax.nn.silu(gate) * up).astype(jnp.bfloat16)
        term = jnp.dot(hidden, w_down, preferred_element_type=jnp.float32).astype(jnp.bfloat16)
        return lax.psum(term, "tp")

    return jax.shard_map(
        step,
        mesh=mesh,
        in_specs=(P("dp", None), P(None, "tp"), P(None, "tp"), P("tp", None)),
        out_specs=P("dp", None),
        check_vma=False,
    )
```

profile of v0, /device:TPU:113, one launch (start us, length us, event | category | flops | bytes accessed | tf_op | source)
XLA Modules:
  0.0 409.8 jit_solution(6283610374328969184)
XLA Ops:
  6.5 0.0 all-reduce.2.cloned.1.call-start
  6.6 52.9 %fusion = f32[2048,2048]{1,0:T(8,128)} fusion(bf16[2048,5120]{1,0:T(8,128)(2,1)} %param.4, bf16[5120,2048]{1,0:T(8,128)(2,1)} %param.5), kind=kOutput, calls=%fused_computation.2 | convolution fusion | flops 42949672960 | bytes 58720256 | tf_op jit(solution)/shard_map/dot_general | solution.py:9
  59.4 58.3 %multiply_convert_fusion = bf16[2048,2048]{1,0:T(8,128)(2,1)} fusion(f32[2048,2048]{1,0:T(8,128)} %fusion, bf16[2048,5120]{1,0:T(8,128)(2,1)} %param.4, bf16[5120,2048]{1,0:T(8,128)(2,1)} %param.6), kind=kOutput, calls=%fused_computation.1 | convolution fusion | flops 42974838784 | bytes 67108864 | tf_op jit(solution)/shard_map/dot_general | solution.py:10
  117.7 51.2 %convolution_convert_fusion = bf16[2048,5120]{1,0:T(8,128)(2,1)} fusion(bf16[2048,2048]{1,0:T(8,128)(2,1)} %multiply_convert_fusion, bf16[2048,5120]{1,0:T(8,128)(2,1)} %param.7), kind=kOutput, calls=%fused_computation | convolution fusion | flops 42960158720 | bytes 50331648 | tf_op jit(solution)/shard_map/dot_general | solution.py:12
  168.9 0.1 all-reduce.2.cloned.1.call-update
  168.9 216.7 %all-reduce.2.cloned.1.call-done = bf16[2048,5120]{1,0:T(8,128)(2,1)} async-done(((bf16[2048,5120]{1,0:T(8,128)(2,1)}), bf16[2048,5120]{1,0:T(8,128)(2,1)}) %all-reduce.2.cloned.1.call-update) | async-done | bytes 20971536 | tf_op jit(solution)/shard_map/psum | solution.py:13
  385.7 17.3 %copy.6 = bf16[2048,5120]{1,0:T(8,128)(2,1)} copy(bf16[2048,5120]{1,0:T(8,128)(2,1)} %all-reduce.2.cloned.1.call-done) | data formatting | bytes 41943040
Async XLA Ops:
  6.5 379.1 %all-reduce.2.cloned.1.call-start = ((), (), s32[]{:S(2)}) async-start(), calls=%async_computation | async-start | bytes 41943040 | tf_op jit(solution)/shard_map/psum | solution.py:13
Sparse Core Ops, SparseCore 0:
  169.1 216.5 all-reduce.1
where the time goes:
time: 410 us
  waiting for transfers between devices  217 us (53%)
  matrix products  162 us (40%)
  local copies, waits for them, and re-layouts  17.3 us (4%)
  between operations  13.4 us (3%)
    psum x1, waiting for transfers between devices, step(): return lax.psum(term, 'tp')  217 us
    dot_general x1, matrix products, step(): up = jnp.dot(x, w_up, preferred_element_type=jnp.float32)  58.3 us
    dot_general x1, matrix products, step(): gate = jnp.dot(x, w_gate, preferred_element_type=jnp.float32)  52.9 us
    dot_general x1, matrix products, step(): jnp.dot(hidden, w_down, preferred_element_type=jnp.float32)  51.2 us
    unnamed x1, local copies, waits for them, and re-layouts  17.3 us
  transfers between devices with their start and end apart: 1, of which 1 were waited for; matrix products, arithmetic and copies ran while one was open for 0% of the time, Pallas kernels for 0%

commit v1 on v0

v1 whole, which is shorter than its diff:
```python
import functools

import jax
import jax.numpy as jnp
from jax import lax
from jax.experimental import pallas as pl
from jax.experimental.pallas import tpu as pltpu
from jax.sharding import PartitionSpec as P

F32 = jnp.float32
BF16 = jnp.bfloat16
CORES = 2
CHUNK = 256
STEPS = 4
SLOTS = 4


def kernel(
    n,
    x_ref, wg_ref, wu_ref, wd_ref,
    y_ref,
    xb, wg, wu, wd, hb, part, sib_s, sib_r, h1_s, h1_r, h2_s, h2_r, fin,
    x_sem, w_sem, wd_sem, sib_ss, sib_rs, h1_ss, h1_rs, h2_ss, h2_rs,
    a1_ss, a1_rs, a2_ss, a2_rs, fw_ss, fw_rs, loc_sem,
):
    chips = n // CORES
    rows, _ = x_ref.shape
    tile = wg.shape[-1]
    width = wd.shape[-1]
    half = CHUNK // CORES
    shard = half // chips
    piece = shard // 2
    chunks = rows // CHUNK
    units = chunks * STEPS

    me = lax.axis_index("tp")
    core = lax.rem(me, CORES)
    chip = me // CORES
    right_chip = lax.rem(chip + 1, chips)
    left_chip = lax.rem(chip + chips - 1, chips)
    far_chip = lax.rem(chip + 2, chips)
    right = right_chip * CORES + core
    left = left_chip * CORES + core
    sib = chip * CORES + (CORES - 1 - core)
    roles = (far_chip, left_chip, right_chip, chip)
    side = (right, left)

    def y_rows(u, owner_chip, owner_core, first=0, count=None):
        base = (u // STEPS) * CHUNK + owner_core * half + owner_chip * shard + first
        count = shard if count is None else count
        return pl.ds(pl.multiple_of(base, 16), count)

    def y_cols(u):
        return pl.ds(pl.multiple_of(lax.rem(u, STEPS) * width, 128), width)

    def slot_of(u):
        return lax.rem(u, SLOTS)

    def w_copies(s):
        k = lax.rem(s, 2)
        cols = pl.ds(pl.multiple_of(lax.rem(s, STEPS) * tile, 128), tile)
        return (
            pltpu.make_async_copy(wg_ref.at[:, cols], wg.at[k], w_sem.at[k, 0]),
            pltpu.make_async_copy(wu_ref.at[:, cols], wu.at[k], w_sem.at[k, 1]),
        )

    def wd_copy(j):
        cols = pl.ds(pl.multiple_of(j * width, 128), width)
        return pltpu.make_async_copy(wd_ref.at[:, cols], wd.at[j], wd_sem.at[j])

    def x_start(k):
        for h in range(CORES):
            owner_core = core if h == 1 else CORES - 1 - core
            for r, owner_chip in enumerate(roles):
                base = k * CHUNK + owner_core * half + owner_chip * shard
                pltpu.make_async_copy(
                    x_ref.at[pl.ds(pl.multiple_of(base, 16), shard)],
                    xb.at[lax.rem(k, 2), pl.ds(h * half + r * shard, shard)],
                    x_sem.at[lax.rem(k, 2)],
                ).start()

    def x_wait(k):
        pltpu.make_async_copy(
            x_ref.at[pl.ds(0, CHUNK)], xb.at[lax.rem(k, 2)], x_sem.at[lax.rem(k, 2)]
        ).wait()

    def remote(src, dst, ss, rs, dev):
        return pltpu.make_async_remote_copy(
            src_ref=src, dst_ref=dst, send_sem=ss, recv_sem=rs,
            device_id={"tp": dev}, device_id_type=pl.DeviceIdType.MESH,
        )

    def sib_copy(u):
        k = slot_of(u)
        return remote(sib_s.at[k], sib_r.at[k], sib_ss.at[k], sib_rs.at[k], sib)

    def h1_copy(u, d):
        k = slot_of(u)
        return remote(h1_s.at[k, d], h1_r.at[k, d], h1_ss.at[k, d], h1_rs.at[k, d], side[d])

    def h2_copy(u, d):
        k = slot_of(u)
        return remote(h2_s.at[k, d], h2_r.at[k, d], h2_ss.at[k, d], h2_rs.at[k, d], side[d])

    def a1_copy(u, d):
        k = slot_of(u)
        dst = y_ref.at[y_rows(u, chip, core), y_cols(u)]
        return remote(fin.at[k], dst, a1_ss.at[k, d], a1_rs.at[k, d], side[d])

    def a2_copy(u, d):
        k = slot_of(u)
        owner = (left_chip, right_chip)[d]
        at = y_ref.at[y_rows(u, owner, core, d * piece, piece), y_cols(u)]
        return remote(at, at, a2_ss.at[k, d], a2_rs.at[k, d], side[d])

    def fw_copy(u):
        k = slot_of(u)
        base = (u // STEPS) * CHUNK + core * half
        at = y_ref.at[pl.ds(pl.multiple_of(base, 16), half), y_cols(u)]
        return remote(at, at, fw_ss.at[k], fw_rs.at[k], sib)

    def loc_copy(u):
        k = slot_of(u)
        dst = y_ref.at[y_rows(u, chip, core), y_cols(u)]
        return pltpu.make_async_copy(fin.at[k], dst, loc_sem.at[k])

    barrier = pltpu.get_barrier_semaphore()
    for dev in (left, right, sib):
        pl.semaphore_signal(
            barrier, inc=1, device_id={"tp": dev}, device_id_type=pl.DeviceIdType.MESH
        )
    x_start(0)
    for c in w_copies(0):
        c.start()
    pl.semaphore_wait(barrier, 3)

    def load(ref, k, r, first=0, count=None):
        return ref[k, pl.ds(r * shard + first, shard if count is None else count)].astype(F32)

    def when(lo, s, hi):
        return pl.when(jnp.logical_and(s >= lo, s < hi))

    @pl.loop(0, units + STEPS + 5)
    def _(s):
        t = s - STEPS

        @pl.when(s < units)
        def _():
            k = s // STEPS

            @pl.when(lax.rem(s, STEPS) == 0)
            def _():
                x_wait(k)

                @pl.when(k + 1 < chunks)
                def _():
                    x_start(k + 1)

        @when(STEPS - 1, s, 2 * STEPS - 1)
        def _():
            wd_copy(s - (STEPS - 1)).start()

        @pl.when(s < units)
        def _():
            for c in w_copies(s):
                c.wait()

            @pl.when(s + 1 < units)
            def _():
                for c in w_copies(s + 1):
                    c.start()

        @when(0, t, units)
        def _():
            @pl.when(t < STEPS)
            def _():
                wd_copy(t).wait()

            k = slot_of(t)
            h = hb[lax.rem(t // STEPS, 2)]
            term = jnp.dot(h, wd[lax.rem(t, STEPS)], preferred_element_type=F32)
            sib_s[k] = term[:half].astype(BF16)
            part[k] = term[half:]
            sib_copy(t).start()

        @pl.when(s < units)
        def _():
            k = lax.rem(s, 2)
            b = lax.rem(s // STEPS, 2)
            xs = xb[b]
            gate = jnp.dot(xs, wg[k], preferred_element_type=F32)
            up = jnp.dot(xs, wu[k], preferred_element_type=F32)
            cols = pl.ds(pl.multiple_of(lax.rem(s, STEPS) * tile, 128), tile)
            hb[b, :, cols] = (jax.nn.silu(gate) * up).astype(BF16)

        @when(0, t, units)
        def _():
            sib_copy(t).wait()
            k = slot_of(t)
            for d in range(2):
                h1_s[k, d] = (
                    load(part, k, 0, d * piece, piece) + load(sib_r, k, 0, d * piece, piece)
                ).astype(BF16)
                h1_copy(t, d).start()

        @when(0, t - 1, units)
        def _():
            u = t - 1
            k = slot_of(u)
            for d in range(2):
                h1_copy(u, d).wait()
            for d in range(2):
                r = (2, 1)[d]
                for p in range(2):
                    v = load(part, k, r, p * piece, piece) + load(sib_r, k, r, p * piece, piece)
                    if p == d:
                        v = v + h1_r[k, d].astype(F32)
                    h2_s[k, d, pl.ds(p * piece, piece)] = v.astype(BF16)
                h2_copy(u, d).start()

        @when(0, t - 2, units)
        def _():
            u = t - 2
            k = slot_of(u)
            for d in range(2):
                h2_copy(u, d).wait()
            v = load(part, k, 3) + load(sib_r, k, 3)
            v = v + h2_r[k, 0].astype(F32) + h2_r[k, 1].astype(F32)
            fin[k] = v.astype(BF16)
            for d in range(2):
                a1_copy(u, d).start()
            loc_copy(u).start()

        @when(0, t - 3, units)
        def _():
            u = t - 3
            for d in range(2):
                a1_copy(u, d).wait()
            for d in range(2):
                a2_copy(u, d).start()
            loc_copy(u).wait()

        @when(0, t - 4, units)
        def _():
            u = t - 4
            for d in range(2):
                a2_copy(u, d).wait()
            fw_copy(u).start()

        @when(0, t - 5, units)
        def _():
            fw_copy(t - 5).wait()


def solution(mesh):
    n = mesh.shape["tp"]

    def step(x, w_gate, w_up, w_down):
        rows, d = x.shape
        f = w_gate.shape[1]
        tile = f // STEPS
        width = d // STEPS
        half = CHUNK // CORES
        shard = half // (n // CORES)
        piece = shard // 2
        dma = pltpu.SemaphoreType.DMA
        any_spec = pl.BlockSpec(memory_space=pltpu.HBM)
        return pl.pallas_call(
            functools.partial(kernel, n),
            out_shape=jax.ShapeDtypeStruct((rows, d), BF16),
            in_specs=[any_spec] * 4,
            out_specs=any_spec,
            scratch_shapes=[
                pltpu.VMEM((2, CHUNK, d), BF16),
                pltpu.VMEM((2, d, tile), BF16),
                pltpu.VMEM((2, d, tile), BF16),
                pltpu.VMEM((STEPS, f, width), BF16),
                pltpu.VMEM((2, CHUNK, f), BF16),
                pltpu.VMEM((SLOTS, half, width), F32),
                pltpu.VMEM((SLOTS, half, width), BF16),
                pltpu.VMEM((SLOTS, half, width), BF16),
                pltpu.VMEM((SLOTS, 2, piece, width), BF16),
                pltpu.VMEM((SLOTS, 2, piece, width), BF16),
                pltpu.VMEM((SLOTS, 2, shard, width), BF16),
                pltpu.VMEM((SLOTS, 2, shard, width), BF16),
                pltpu.VMEM((SLOTS, shard, width), BF16),
                dma((2,)),
                dma((2, 2)),
                dma((STEPS,)),
                dma((SLOTS,)),
                dma((SLOTS,)),
                dma((SLOTS, 2)),
                dma((SLOTS, 2)),
                dma((SLOTS, 2)),
                dma((SLOTS, 2)),
                dma((SLOTS, 2)),
                dma((SLOTS, 2)),
                dma((SLOTS, 2)),
                dma((SLOTS, 2)),
                dma((SLOTS,)),
                dma((SLOTS,)),
                dma((SLOTS,)),
            ],
            compiler_params=pltpu.CompilerParams(
                collective_id=0, has_side_effects=True, vmem_limit_bytes=67_043_328
            ),
            name="mlp_ring",
        )(x, w_gate, w_up, w_down)

    return jax.shard_map(
        step,
        mesh=mesh,
        in_specs=(P("dp", None), P(None, "tp"), P(None, "tp"), P("tp", None)),
        out_specs=P("dp", None),
        check_vma=False,
    )
```

time: 410 us -> 239 us (0.58)
  Pallas kernels: 0 us -> 222 us
  waiting for transfers between devices: 217 us -> 0 us
  matrix products: 162 us -> 0 us
  between operations: 13.4 us -> 0.01 us
    pallas_call x0 -> x1, Pallas kernels: none -> 222 us  [step(): pl.pallas_call(functools.partial(kernel, n), out_shape=jax.ShapeDtypeStru...]
    psum x1 -> x0, waiting for transfers between devices: 217 us -> none  [step(): return lax.psum(term, 'tp')]
    dot_general x3 -> x0, matrix products: 162 us -> none  [the longest x1 58.3 us: step(): up = jnp.dot(x, w_up, preferred_element_type=jnp.float32)]
  transfers between devices with their start and end apart: 1 -> 0, of which waited for: 1 -> 0; matrix products, arithmetic and copies ran while one was open for 0% -> 0% of each run, Pallas kernels for 0% -> 0%
where the time goes in v1:
time: 239 us
  Pallas kernels  222 us (93%)
  local copies, waits for them, and re-layouts  17.3 us (7%)
    pallas_call x1, Pallas kernels, step(): pl.pallas_call(functools.partial(kernel, n), out_shape=jax.ShapeDtypeStru...  222 us
    unnamed x1, local copies, waits for them, and re-layouts  17.3 us

profile of v1, /device:TPU:113, one launch (start us, length us, event | category | flops | bytes accessed | tf_op | source)
XLA Modules:
  0.0 239.0 jit_solution(3458883253128637057)
XLA Ops:
  0.0 221.7 %mlp_ring.1 = bf16[2048,5120]{1,0:T(8,128)(2,1)} custom-call(bf16[2048,5120]{1,0:T(8,128)(2,1)} %x_ref.1, bf16[5120,2048]{1,0:T(8,128)(2,1)} %wg_ref.1, bf16[5120,2048]{1,0:T(8,128)(2,1)} %wu_ref.1, bf16[2048,5120]{1,0:T(8,128)(2,1)} %wd_ref.1), custom_call_target="tpu_custom_call" | custom-call | tf_op jit(solution)/shard_map/mlp_ring/pallas_call | solution.py:268
  221.7 17.3 %copy.6 = bf16[2048,5120]{1,0:T(8,128)(2,1)} copy(bf16[2048,5120]{1,0:T(8,128)(2,1)} %mlp_ring.1) | data formatting | bytes 41943040

commit v2 on v0

v2 whole, which is shorter than its diff:
```python
import functools

import jax
import jax.numpy as jnp
from jax import lax
from jax.experimental import pallas as pl
from jax.experimental.pallas import tpu as pltpu
from jax.sharding import PartitionSpec as P

F32 = jnp.float32
BF16 = jnp.bfloat16
CORES = 2
CHUNK = 256
UNITS = 4
TILES = 8
POINTS = UNITS + TILES
W_SLOTS = 4
LAG_FAR, LAG_NEAR, LAG_OWN, LAG_ON, LAG_SIB, LAG_END = 1, 5, 9, 13, 17, 21


def kernel(
    n,
    x_ref, wg_ref, wu_ref, wd_ref,
    y_ref, wd,
    xb, wb, hb, part, sib_s, sib_r, h1_s, h1_r, h2_s, h2_r, fin,
    x_sem, w_sem, wd_sem, sib_ss, sib_rs, h1_ss, h1_rs, h2_ss, h2_rs,
    a1_ss, a1_rs, a2_ss, a2_rs, fw_ss, fw_rs, loc_sem, in_sem,
):
    chips = n // CORES
    rows, _ = x_ref.shape
    tile = wb.shape[-1] // 2
    width = wd.shape[-1]
    half = CHUNK // CORES
    shard = half // chips
    piece = shard // 2
    chunks = rows // CHUNK

    me = lax.axis_index("tp")
    core = lax.rem(me, CORES)
    chip = me // CORES
    right_chip = lax.rem(chip + 1, chips)
    left_chip = lax.rem(chip + chips - 1, chips)
    far_chip = lax.rem(chip + 2, chips)
    sib = chip * CORES + (CORES - 1 - core)
    roles = (far_chip, left_chip, right_chip, chip)
    side = (right_chip * CORES + core, left_chip * CORES + core)

    def y_at(ref, k, i, owner_chip, first=0, count=None):
        base = k * CHUNK + core * half + owner_chip * shard + first
        count = shard if count is None else count
        return ref.at[i, pl.ds(pl.multiple_of(base, 16), count)]

    def by_chunk(k, body):
        @pl.when(k < chunks - 1)
        def _():
            body(y_ref)

        @pl.when(k == chunks - 1)
        def _():
            body(wd)

    def w_copies(w):
        k = w % W_SLOTS
        cols = pl.ds((w % TILES) * tile, tile)
        return (
            pltpu.make_async_copy(wg_ref.at[:, cols], wb.at[k, :, pl.ds(0, tile)], w_sem.at[k, 0]),
            pltpu.make_async_copy(wu_ref.at[:, cols], wb.at[k, :, pl.ds(tile, tile)], w_sem.at[k, 1]),
        )

    def w_start(w):
        for c in w_copies(w):
            c.start()

    def wd_copy(i):
        cols = pl.ds(i * width, width)
        return pltpu.make_async_copy(wd_ref.at[:, cols], wd.at[i], wd_sem.at[i])

    def x_start(k):
        for h in range(CORES):
            owner_core = core if h == 1 else CORES - 1 - core
            for r, owner_chip in enumerate(roles):
                base = k * CHUNK + owner_core * half + owner_chip * shard
                pltpu.make_async_copy(
                    x_ref.at[pl.ds(pl.multiple_of(base, 16), shard)],
                    xb.at[pl.ds(h * half + r * shard, shard)],
                    x_sem.at[0],
                ).start()

    def x_wait():
        pltpu.make_async_copy(x_ref.at[pl.ds(0, CHUNK)], xb, x_sem.at[0]).wait()

    def remote(src, dst, ss, rs, dev):
        return pltpu.make_async_remote_copy(
            src_ref=src, dst_ref=dst, send_sem=ss, recv_sem=rs,
            device_id={"tp": dev}, device_id_type=pl.DeviceIdType.MESH,
        )

    def sib_copy(i):
        return remote(sib_s.at[i], sib_r.at[i], sib_ss.at[i], sib_rs.at[i], sib)

    def h1_copy(i, d):
        return remote(h1_s.at[i, d], h1_r.at[i, d], h1_ss.at[i, d], h1_rs.at[i, d], side[d])

    def h2_copy(i, d):
        return remote(h2_s.at[i, d], h2_r.at[i, d], h2_ss.at[i, d], h2_rs.at[i, d], side[d])

    def a1_copy(ref, k, i, d):
        return remote(fin.at[i], y_at(ref, k, i, chip), a1_ss.at[i, d], a1_rs.at[i, d], side[d])

    def a2_copy(ref, k, i, d):
        at = y_at(ref, k, i, (left_chip, right_chip)[d], d * piece, piece)
        return remote(at, at, a2_ss.at[i, d], a2_rs.at[i, d], side[d])

    def fw_copy(ref, k, i):
        at = y_at(ref, k, i, 0, 0, half)
        p = lax.rem(k, 2)
        return remote(at, at, fw_ss.at[p, i], fw_rs.at[p, i], sib)

    def loc_copy(k, i):
        return pltpu.make_async_copy(fin.at[i], y_at(y_ref, k, i, chip), loc_sem.at[i])

    early = pl.ds(0, (chunks - 2) * CHUNK)
    late = pl.ds((chunks - 2) * CHUNK, CHUNK)

    def in_copy(i, at, p):
        return pltpu.make_async_copy(y_ref.at[i, at], wd.at[i, at], in_sem.at[p, i])

    barrier = pltpu.get_barrier_semaphore()
    for dev in (*side, sib):
        pl.semaphore_signal(
            barrier, inc=1, device_id={"tp": dev}, device_id_type=pl.DeviceIdType.MESH
        )
    x_start(0)
    for w in range(W_SLOTS - 1):
        w_start(w)
    pl.semaphore_wait(barrier, 3)

    def load(ref, i, r, first=0, count=None):
        return ref[i, pl.ds(r * shard + first, shard if count is None else count)].astype(F32)

    def point(k, c):
        if c < UNITS:
            @pl.when(jnp.logical_and(k >= 0, k < chunks))
            def _():
                @pl.when(k == 0)
                def _():
                    wd_copy(c).wait()

                if c == 0:

                    @pl.when(k + 1 < chunks)
                    def _():
                        x_start(k + 1)

                term = jnp.dot(hb[...], wd[c], preferred_element_type=F32)
                sib_s[c] = term[:half].astype(BF16)
                part[c] = term[half:]
                sib_copy(c).start()
        else:
            j = c - UNITS

            @pl.when(k + 1 < chunks)
            def _():
                if j == 0:
                    x_wait()
                for cp in w_copies(j):
                    cp.wait()
                if j == TILES - W_SLOTS + 1:

                    @pl.when(k < 0)
                    def _():
                        for i in range(UNITS):
                            wd_copy(i).start()

                if j < TILES - W_SLOTS + 1:
                    w_start(j + W_SLOTS - 1)
                else:

                    @pl.when(k + 2 < chunks)
                    def _():
                        w_start(j + W_SLOTS - 1)

                both = jnp.dot(xb[...], wb[j % W_SLOTS], preferred_element_type=F32)
                cols = pl.ds(j * tile, tile)
                hb[:, cols] = (jax.nn.silu(both[:, :tile]) * both[:, tile:]).astype(BF16)

        def stage(lag):
            i = (c - lag) % POINTS
            q = k + (c - lag) // POINTS

            def run(body):
                if i < UNITS:

                    @pl.when(jnp.logical_and(q >= 0, q < chunks))
                    def _():
                        body(q, i)

            return run

        @stage(LAG_FAR)
        def _(q, i):
            sib_copy(i).wait()
            for d in range(2):
                h1_s[i, d] = (
                    load(part, i, 0, d * piece, piece) + load(sib_r, i, 0, d * piece, piece)
                ).astype(BF16)
                h1_copy(i, d).start()
            for r in range(1, 4):
                part[i, pl.ds(r * shard, shard)] = load(part, i, r) + load(sib_r, i, r)

        @stage(LAG_NEAR)
        def _(q, i):
            for d in range(2):
                h1_copy(i, d).wait()
            for d in range(2):
                r = (2, 1)[d]
                h2_s[i, d, pl.ds(d * piece, piece)] = (
                    load(part, i, r, d * piece, piece) + h1_r[i, d].astype(F32)
                ).astype(BF16)
                h2_s[i, d, pl.ds((1 - d) * piece, piece)] = load(
                    part, i, r, (1 - d) * piece, piece
                ).astype(BF16)
                h2_copy(i, d).start()

        @stage(LAG_OWN)
        def _(q, i):
            for d in range(2):
                h2_copy(i, d).wait()
            v = load(part, i, 3) + h2_r[i, 0].astype(F32) + h2_r[i, 1].astype(F32)
            fin[i] = v.astype(BF16)

            def go(ref):
                for d in range(2):
                    a1_copy(ref, q, i, d).start()

            by_chunk(q, go)

            @pl.when(q < chunks - 1)
            def _():
                loc_copy(q, i).start()

            @pl.when(q == chunks - 1)
            def _():
                at = pl.ds(pl.multiple_of(q * CHUNK + core * half + chip * shard, 16), shard)
                wd[i, at] = v.astype(BF16)

        @stage(LAG_ON)
        def _(q, i):
            def go(ref):
                for d in range(2):
                    a1_copy(ref, q, i, d).wait()
                for d in range(2):
                    a2_copy(ref, q, i, d).start()

            by_chunk(q, go)

            @pl.when(q < chunks - 1)
            def _():
                loc_copy(q, i).wait()

        @stage(LAG_SIB)
        def _(q, i):
            def go(ref):
                for d in range(2):
                    a2_copy(ref, q, i, d).wait()
                fw_copy(ref, q, i).start()

            by_chunk(q, go)

        @stage(LAG_END)
        def _(q, i):
            by_chunk(q, lambda ref: fw_copy(ref, q, i).wait())

            @pl.when(q == chunks - 2)
            def _():
                in_copy(i, late, 1).start()

        if c == UNITS:
            @pl.when(k == chunks - 1)
            def _():
                for i in range(UNITS):
                    in_copy(i, early, 0).start()

    for c in range(UNITS, POINTS):
        point(jnp.int32(-1), c)

    @pl.loop(0, chunks + LAG_END // POINTS + 1)
    def _(k):
        for c in range(POINTS):
            point(k, c)

    for i in range(UNITS):
        in_copy(i, early, 0).wait()
        in_copy(i, late, 1).wait()


def write_out(v_ref, y_ref, sem):
    width = v_ref.shape[-1]
    copies = [
        pltpu.make_async_copy(v_ref.at[i], y_ref.at[:, pl.ds(i * width, width)], sem.at[i])
        for i in range(UNITS)
    ]
    for c in copies:
        c.start()
    for c in copies:
        c.wait()


def solution(mesh):
    n = mesh.shape["tp"]

    def step(x, w_gate, w_up, w_down):
        rows, d = x.shape
        f = w_gate.shape[1]
        tile = f // TILES
        width = d // UNITS
        half = CHUNK // CORES
        shard = half // (n // CORES)
        piece = shard // 2
        dma = pltpu.SemaphoreType.DMA
        hbm = pl.BlockSpec(memory_space=pltpu.HBM)
        vmem = pl.BlockSpec(memory_space=pltpu.VMEM)
        assert rows == f
        _, y = pl.pallas_call(
            functools.partial(kernel, n),
            out_shape=(
                jax.ShapeDtypeStruct((UNITS, rows, width), BF16),
                pltpu.VMEM((UNITS, f, width), BF16),
            ),
            in_specs=[hbm] * 4,
            out_specs=(hbm, vmem),
            scratch_shapes=[
                pltpu.VMEM((CHUNK, d), BF16),
                pltpu.VMEM((W_SLOTS, d, 2 * tile), BF16),
                pltpu.VMEM((CHUNK, f), BF16),
                pltpu.VMEM((UNITS, half, width), F32),
                pltpu.VMEM((UNITS, half, width), BF16),
                pltpu.VMEM((UNITS, half, width), BF16),
                pltpu.VMEM((UNITS, 2, piece, width), BF16),
                pltpu.VMEM((UNITS, 2, piece, width), BF16),
                pltpu.VMEM((UNITS, 2, shard, width), BF16),
                pltpu.VMEM((UNITS, 2, shard, width), BF16),
                pltpu.VMEM((UNITS, shard, width), BF16),
                dma((1,)),
                dma((W_SLOTS, 2)),
                dma((UNITS,)),
                dma((UNITS,)),
                dma((UNITS,)),
                *[dma((UNITS, 2))] * 8,
                dma((2, UNITS)),
                dma((2, UNITS)),
                dma((UNITS,)),
                dma((2, UNITS)),
            ],
            compiler_params=pltpu.CompilerParams(
                collective_id=0, has_side_effects=True, vmem_limit_bytes=42 << 20
            ),
            name="mlp_ring",
        )(x, w_gate, w_up, w_down)
        return pl.pallas_call(
            write_out,
            out_shape=jax.ShapeDtypeStruct((rows, d), BF16),
            in_specs=[vmem],
            out_specs=hbm,
            scratch_shapes=[dma((UNITS,))],
            compiler_params=pltpu.CompilerParams(vmem_limit_bytes=1 << 20),
            name="write_out",
        )(y)

    return jax.shard_map(
        step,
        mesh=mesh,
        in_specs=(P("dp", None), P(None, "tp"), P(None, "tp"), P("tp", None)),
        out_specs=P("dp", None),
        check_vma=False,
    )
```

time: 410 us -> 209 us (0.51)
  waiting for transfers between devices: 217 us -> 0 us
  Pallas kernels: 0 us -> 209 us
  matrix products: 162 us -> 0 us
  local copies, waits for them, and re-layouts: 17.3 us -> 0 us
  between operations: 13.4 us -> 0.17 us
    psum x1 -> x0, waiting for transfers between devices: 217 us -> none  [step(): return lax.psum(term, 'tp')]
    pallas_call x0 -> x2, Pallas kernels: none -> 209 us  [the longest x1 201 us: step(): pl.pallas_call(functools.partial(kernel, n), out_shape=(jax.ShapeDtypeStr...]
    dot_general x3 -> x0, matrix products: 162 us -> none  [the longest x1 58.3 us: step(): up = jnp.dot(x, w_up, preferred_element_type=jnp.float32)]
    unnamed x1 -> x0, local copies, waits for them, and re-layouts: 17.3 us -> none
  transfers between devices with their start and end apart: 1 -> 0, of which waited for: 1 -> 0; matrix products, arithmetic and copies ran while one was open for 0% -> 0% of each run, Pallas kernels for 0% -> 0%
where the time goes in v2:
time: 209 us
  Pallas kernels  209 us (100%)
    pallas_call x1, Pallas kernels, step(): pl.pallas_call(functools.partial(kernel, n), out_shape=(jax.ShapeDtypeStr...  201 us
    pallas_call x1, Pallas kernels, step(): pl.pallas_call(write_out, out_shape=jax.ShapeDtypeStruct((rows, d), BF16)...  7.27 us

profile of v2, /device:TPU:113, one launch (start us, length us, event | category | flops | bytes accessed | tf_op | source)
XLA Modules:
  0.0 208.8 jit_solution(14764104235009083347)
XLA Ops:
  0.0 201.3 %mlp_ring.1 = (bf16[4,2048,1280]{2,1,0:T(8,128)(2,1)}, bf16[4,2048,1280]{2,1,0:T(8,128)(2,1)S(1)}) custom-call(bf16[2048,5120]{1,0:T(8,128)(2,1)} %x_ref.1, bf16[5120,2048]{1,0:T(8,128)(2,1)} %wg_ref.1, bf16[5120,2048]{1,0:T(8,128)(2,1)} %wu_ref.1, bf16[2048,5120]{1,0:T(8,128)(2,1)} %wd_ref.1), custom_call_target="tpu_custom_call" | custom-call | tf_op jit(solution)/shard_map/mlp_ring/pallas_call | solution.py:324
  201.3 7.3 %write_out.1 = bf16[2048,5120]{1,0:T(8,128)(2,1)} custom-call(bf16[4,2048,1280]{2,1,0:T(8,128)(2,1)S(1)} %get-tuple-element.6.v_ref), custom_call_target="tpu_custom_call" | custom-call | tf_op jit(solution)/shard_map/write_out/pallas_call | solution.py:360

commit v3 on v2

--- a/solution.py
+++ b/solution.py
@@ -15,7 +15,7 @@
 TILES = 8
 POINTS = UNITS + TILES
 W_SLOTS = 4
-LAG_FAR, LAG_NEAR, LAG_OWN, LAG_ON, LAG_SIB, LAG_END = 1, 5, 9, 13, 17, 21
+LAG_FAR, LAG_NEAR, LAG_OWN, LAG_ON, LAG_SIB, LAG_END = (1, 1), (5, 5), (9, 9), (13, 13), (17, 17), (21, 21)
 
 
 def kernel(
@@ -131,24 +131,39 @@
             barrier, inc=1, device_id={"tp": dev}, device_id_type=pl.DeviceIdType.MESH
         )
     x_start(0)
-    for w in range(W_SLOTS - 1):
-        w_start(w)
-    pl.semaphore_wait(barrier, 3)
+    w_start(0)
+    x_wait()
+    w_start(1)
+    w_start(2)
 
     def load(ref, i, r, first=0, count=None):
         return ref[i, pl.ds(r * shard + first, shard if count is None else count)].astype(F32)
 
+    def when(cond):
+        if isinstance(cond, bool):
+            return (lambda body: body()) if cond else (lambda body: None)
+        return pl.when(cond)
+
+    def within(lo, q, hi):
+        if isinstance(q, int):
+            return False if q < lo else q < hi
+        return jnp.logical_and(q >= lo, q < hi)
+
     def point(k, c):
         if c < UNITS:
-            @pl.when(jnp.logical_and(k >= 0, k < chunks))
-            def _():
-                @pl.when(k == 0)
+            @when(within(0, k, chunks))
+            def _():
+                @when(k == 0)
                 def _():
                     wd_copy(c).wait()
+                    if c + 3 < UNITS:
+                        wd_copy(c + 3).start()
+                    else:
+                        w_start(TILES + c + 3 - UNITS)
 
                 if c == 0:
 
-                    @pl.when(k + 1 < chunks)
+                    @when(k + 1 < chunks)
                     def _():
                         x_start(k + 1)
 
@@ -159,45 +174,63 @@
         else:
             j = c - UNITS
 
-            @pl.when(k + 1 < chunks)
+            @when(k + 1 < chunks)
             def _():
                 if j == 0:
-                    x_wait()
+
+                    @when(k >= 0)
+                    def _():
+                        x_wait()
+
                 for cp in w_copies(j):
                     cp.wait()
-                if j == TILES - W_SLOTS + 1:
-
-                    @pl.when(k < 0)
+
+                @when(k < 0)
+                def _():
+                    if j + 3 < TILES:
+                        w_start(j + 3)
+                    else:
+                        wd_copy(j + 3 - TILES).start()
+
+                ahead = j + W_SLOTS - 1
+                if ahead < TILES:
+
+                    @when(k >= 0)
                     def _():
-                        for i in range(UNITS):
-                            wd_copy(i).start()
-
-                if j < TILES - W_SLOTS + 1:
-                    w_start(j + W_SLOTS - 1)
+                        w_start(ahead)
                 else:
 
-                    @pl.when(k + 2 < chunks)
+                    @when(within(0, k, chunks - 2))
                     def _():
-                        w_start(j + W_SLOTS - 1)
+                        w_start(ahead)
 
                 both = jnp.dot(xb[...], wb[j % W_SLOTS], preferred_element_type=F32)
                 cols = pl.ds(j * tile, tile)
                 hb[:, cols] = (jax.nn.silu(both[:, :tile]) * both[:, tile:]).astype(BF16)
 
-        def stage(lag):
-            i = (c - lag) % POINTS
-            q = k + (c - lag) // POINTS
-
+        def stage(lag, first):
             def run(body):
-                if i < UNITS:
-
-                    @pl.when(jnp.logical_and(q >= 0, q < chunks))
+                for points, early_unit in ((first, True), (lag, False)):
+                    i = (c - points) % POINTS
+                    q = k + (c - points) // POINTS
+                    if i >= UNITS:
+                        continue
+                    if first == lag:
+                        on = within(0, q, chunks)
+                        if early_unit:
+                            continue
+                    elif early_unit:
+                        on = q == 0
+                    else:
+                        on = within(1, q, chunks)
+
+                    @when(on)
                     def _():
                         body(q, i)
 
             return run
 
-        @stage(LAG_FAR)
+        @stage(*LAG_FAR)
         def _(q, i):
             sib_copy(i).wait()
             for d in range(2):
@@ -208,7 +241,7 @@
             for r in range(1, 4):
                 part[i, pl.ds(r * shard, shard)] = load(part, i, r) + load(sib_r, i, r)
 
-        @stage(LAG_NEAR)
+        @stage(*LAG_NEAR)
         def _(q, i):
             for d in range(2):
                 h1_copy(i, d).wait()
@@ -222,7 +255,7 @@
                 ).astype(BF16)
                 h2_copy(i, d).start()
 
-        @stage(LAG_OWN)
+        @stage(*LAG_OWN)
         def _(q, i):
             for d in range(2):
                 h2_copy(i, d).wait()
@@ -235,16 +268,16 @@
 
             by_chunk(q, go)
 
-            @pl.when(q < chunks - 1)
+            @when(q < chunks - 1)
             def _():
                 loc_copy(q, i).start()
 
-            @pl.when(q == chunks - 1)
+            @when(q == chunks - 1)
             def _():
                 at = pl.ds(pl.multiple_of(q * CHUNK + core * half + chip * shard, 16), shard)
                 wd[i, at] = v.astype(BF16)
 
-        @stage(LAG_ON)
+        @stage(*LAG_ON)
         def _(q, i):
             def go(ref):
                 for d in range(2):
@@ -254,11 +287,11 @@
 
             by_chunk(q, go)
 
-            @pl.when(q < chunks - 1)
+            @when(q < chunks - 1)
             def _():
                 loc_copy(q, i).wait()
 
-        @stage(LAG_SIB)
+        @stage(*LAG_SIB)
         def _(q, i):
             def go(ref):
                 for d in range(2):
@@ -267,24 +300,26 @@
 
             by_chunk(q, go)
 
-        @stage(LAG_END)
+        @stage(*LAG_END)
         def _(q, i):
             by_chunk(q, lambda ref: fw_copy(ref, q, i).wait())
 
-            @pl.when(q == chunks - 2)
+            @when(q == chunks - 2)
             def _():
                 in_copy(i, late, 1).start()
 
         if c == UNITS:
-            @pl.when(k == chunks - 1)
+            @when(k == chunks - 1)
             def _():
                 for i in range(UNITS):
                     in_copy(i, early, 0).start()
 
     for c in range(UNITS, POINTS):
-        point(jnp.int32(-1), c)
-
-    @pl.loop(0, chunks + LAG_END // POINTS + 1)
+        point(-1, c)
+
+    pl.semaphore_wait(barrier, 3)
+
+    @pl.loop(0, chunks + LAG_END[0] // POINTS + 1)
     def _(k):
         for c in range(POINTS):
             point(k, c)

time: 209 us -> 206 us (0.986)
  Pallas kernels: 209 us -> 206 us
    pallas_call x1, Pallas kernels: 201 us -> 198 us  [step(): pl.pallas_call(functools.partial(kernel, n), out_shape=(jax.ShapeDtypeStr...]
where the time goes in v3:
time: 206 us
  Pallas kernels  206 us (100%)
    pallas_call x1, Pallas kernels, step(): pl.pallas_call(functools.partial(kernel, n), out_shape=(jax.ShapeDtypeStr...  198 us
    pallas_call x1, Pallas kernels, step(): pl.pallas_call(write_out, out_shape=jax.ShapeDtypeStruct((rows, d), BF16)...  7.27 us

profile of v3, /device:TPU:113, one launch (start us, length us, event | category | flops | bytes accessed | tf_op | source)
XLA Modules:
  0.0 205.7 jit_solution(14230366791923463579)
XLA Ops:
  0.0 198.3 %mlp_ring.1 = (bf16[4,2048,1280]{2,1,0:T(8,128)(2,1)}, bf16[4,2048,1280]{2,1,0:T(8,128)(2,1)S(1)}) custom-call(bf16[2048,5120]{1,0:T(8,128)(2,1)} %x_ref.1, bf16[5120,2048]{1,0:T(8,128)(2,1)} %wg_ref.1, bf16[5120,2048]{1,0:T(8,128)(2,1)} %wu_ref.1, bf16[2048,5120]{1,0:T(8,128)(2,1)} %wd_ref.1), custom_call_target="tpu_custom_call" | custom-call | tf_op jit(solution)/shard_map/mlp_ring/pallas_call | solution.py:359
  198.3 7.3 %write_out.1 = bf16[2048,5120]{1,0:T(8,128)(2,1)} custom-call(bf16[4,2048,1280]{2,1,0:T(8,128)(2,1)S(1)} %get-tuple-element.6.v_ref), custom_call_target="tpu_custom_call" | custom-call | tf_op jit(solution)/shard_map/write_out/pallas_call | solution.py:395

commit v4 on v3

--- a/solution.py
+++ b/solution.py
@@ -15,7 +15,7 @@
 TILES = 8
 POINTS = UNITS + TILES
 W_SLOTS = 4
-LAG_FAR, LAG_NEAR, LAG_OWN, LAG_ON, LAG_SIB, LAG_END = (1, 1), (5, 5), (9, 9), (13, 13), (17, 17), (21, 21)
+LAG_FAR, LAG_NEAR, LAG_OWN, LAG_ON, LAG_SIB, LAG_END = (1, 1), (5, 4), (9, 8), (13, 12), (17, 17), (21, 21)
 
 
 def kernel(

time: 206 us -> 205 us (level)
  no operation moved by 1% of the time
where the time goes in v4:
time: 205 us
  Pallas kernels  205 us (100%)
    pallas_call x1, Pallas kernels, step(): pl.pallas_call(functools.partial(kernel, n), out_shape=(jax.ShapeDtypeStr...  198 us
    pallas_call x1, Pallas kernels, step(): pl.pallas_call(write_out, out_shape=jax.ShapeDtypeStruct((rows, d), BF16)...  7.27 us

profile of v4, /device:TPU:113, one launch (start us, length us, event | category | flops | bytes accessed | tf_op | source)
XLA Modules:
  0.0 205.0 jit_solution(7536940156751459390)
XLA Ops:
  0.0 197.5 %mlp_ring.1 = (bf16[4,2048,1280]{2,1,0:T(8,128)(2,1)}, bf16[4,2048,1280]{2,1,0:T(8,128)(2,1)S(1)}) custom-call(bf16[2048,5120]{1,0:T(8,128)(2,1)} %x_ref.1, bf16[5120,2048]{1,0:T(8,128)(2,1)} %wg_ref.1, bf16[5120,2048]{1,0:T(8,128)(2,1)} %wu_ref.1, bf16[2048,5120]{1,0:T(8,128)(2,1)} %wd_ref.1), custom_call_target="tpu_custom_call" | custom-call | tf_op jit(solution)/shard_map/mlp_ring/pallas_call | solution.py:359
  197.5 7.3 %write_out.1 = bf16[2048,5120]{1,0:T(8,128)(2,1)} custom-call(bf16[4,2048,1280]{2,1,0:T(8,128)(2,1)S(1)} %get-tuple-element.6.v_ref), custom_call_target="tpu_custom_call" | custom-call | tf_op jit(solution)/shard_map/write_out/pallas_call | solution.py:395
